TPU v7x, 256 devices: a whole 4x4x8 slice. The times are simulated.
256 devices in a mesh: seq: 4 (over y), tp: 8 (over z), grp: 8 (over x, core).
Axes of the slice: x: 4, y: 4, z: 8, core: 2. Of those that a mesh axis runs over, the one named last changes fastest.
Arguments:
- queries: bfloat16 [16, 64, 128], P('grp', 'tp'), may hold values from -2000 to 2000
- cache_pool: bfloat16 [2048, 8, 2, 128, 128], P(('seq', 'grp'), 'tp'), may hold values from -6 to 6
- block_scale: bfloat16 [2048, 8, 2], P(('seq', 'grp'), 'tp'), may hold values from 0.29 to 3
- block_table: int32 [16, 128], replicated, may hold values from 0 to 2047, as said below
- lengths: int32 [16], replicated, may hold values from 128 to 16384
- output_weight: bfloat16 [8192, 8192], P('tp', ('seq', 'grp')), may hold values from -0.0625 to 0.0625
Outputs:
- attention_output: bfloat16 [16, 8192], P('tp', ('seq', 'grp'))
- decode_cache: bfloat16 [16, 128, 8, 2, 128, 128], P('grp', 'seq', 'tp')
- decode_scale: bfloat16 [16, 128, 8, 2], P('grp', 'seq', 'tp')
Inputs may be any that keep to these rules, and one draw needn't show every extreme that they name: block_table names every pool slot exactly once. Take any run of 64 slots starting at a multiple of 64, any group of 2 consecutive requests starting at a multiple of 2, and any range of 32 block positions starting at a multiple of 32: exactly 2 slots of the run hold blocks of those requests at those positions.
All inputs are finite; a program needn't handle non-finite values.
Results may differ from a plain program's by a relative error of at most 0.014.
Values may be sent and summed in bfloat16 or wider, within the bound.
No kernel may reach another device: no remote copies, remote signals or barrier semaphores. Data moves between devices by JAX's collectives and lax.ppermute only.
A program may use at most 64 MiB of HBM per device.

v0:
```python
import math

import jax
import jax.numpy as jnp
from jax import lax
from jax.sharding import PartitionSpec as P

absent_score = -1e30


def sent_to_all(array, axis):
    length = lax.axis_size(axis)
    return lax.all_to_all(
        jnp.broadcast_to(array[None], (length, *array.shape)), axis, 0, 0, tiled=True
    )


def gathered_once(array, axis):
    leaves = jax.tree.leaves(array)
    sequence = sorted(range(len(leaves)), key=lambda k: -leaves[k].size)
    width = (1, *leaves[sequence[0]].shape)[-1]
    lines = [
        jnp.pad(leaves[k].reshape(-1), (0, -leaves[k].size % width)).reshape(-1, width)
        for k in sequence
    ]
    both, at, found = (sent_to_all(jnp.concatenate(lines), axis), 0, {})
    for k, line in zip(sequence, lines):
        share = both[:, at : at + len(line)].reshape(len(both), -1)
        found[k] = share[:, : leaves[k].size].reshape(-1, *leaves[k].shape)
        at += len(line)
    numbers = iter(range(len(leaves)))
    return jax.tree.map(lambda _: found[next(numbers)], array)


def joined_by_halves(pieces, combine):
    while len(jax.tree.leaves(pieces)[0]) > 1:
        pieces = jax.vmap(combine)(
            *(jax.tree.map(lambda part: part[side::2], pieces) for side in (0, 1))
        )
    return jax.tree.map(lambda part: part[0], pieces)


def joined_all(array, axis, combine):
    pieces = gathered_once(array, axis)
    return joined_by_halves(pieces, combine)


def in_order(pieces, dim):
    pieces = jnp.moveaxis(pieces, 0, dim)
    dims = pieces.shape
    return pieces.reshape(*dims[:dim], dims[dim] * dims[dim + 1], *dims[dim + 2 :])


def gather_directly(array, axis, dim):
    pieces = sent_to_all(array, axis)
    return in_order(pieces, dim)


def in_blocks(array, dim, length):
    dims = array.shape
    pieces = array.reshape(*dims[:dim], length, dims[dim] // length, *dims[dim + 1 :])
    return jnp.moveaxis(pieces, dim, 0)


def sum_at_owner(array, axis, dim):
    pieces = in_blocks(array, dim, lax.axis_size(axis))
    arrived = lax.all_to_all(pieces, axis, split_axis=0, concat_axis=0, tiled=True)
    return arrived.sum(axis=0)


def block_scores(block_queries, key_rows, key_scale, live_mask, root_scale):
    scores = jnp.einsum(
        "nkgd,nktd->nkgt", block_queries, key_rows, preferred_element_type=jnp.float32
    )
    scores = scores * key_scale[:, :, None, None] * root_scale
    return jnp.where(live_mask[:, None, None, :], scores, absent_score)


def block_terms(scores, peak_rows, live_mask, value_rows, value_scale):
    weight = jnp.where(live_mask[:, None, None, :], jnp.exp(scores - peak_rows[..., None]), 0.0)
    weight_sum = jnp.sum(weight, axis=-1)
    scaled = (weight * value_scale[:, :, None, None]).astype(jnp.bfloat16)
    partial_sum = jnp.einsum(
        "nkgt,nktd->nkgd", scaled, value_rows, preferred_element_type=jnp.float32
    )
    return (weight_sum, partial_sum)


def combine(former, latter):
    peak_former, sum_former, accum_former = former
    peak_latter, sum_latter, accum_latter = latter
    peak_both = jnp.maximum(peak_former, peak_latter)
    factor_former = jnp.exp(peak_former - peak_both)
    factor_latter = jnp.exp(peak_latter - peak_both)
    return (
        peak_both,
        sum_former * factor_former + sum_latter * factor_latter,
        accum_former * factor_former[..., None] + accum_latter * factor_latter[..., None],
    )


def per_device(queries, cache_pool, block_scale, block_table, lengths, output_weight):
    seq_count = lax.axis_size("seq")
    group_count = lax.axis_size("grp")
    seq_index = lax.axis_index("seq")
    group_index = lax.axis_index("grp")
    sources = seq_count * group_count
    pool_slots = cache_pool.shape[0]
    key_heads = cache_pool.shape[1]
    block_size = cache_pool.shape[3]
    head_size = cache_pool.shape[4]
    batch_rows, table_width = block_table.shape
    per_group = batch_rows // group_count
    share_blocks = table_width // seq_count
    capacity = pool_slots // sources
    heads_here = queries.shape[1]
    groups = heads_here // key_heads
    root_scale = 1.0 / math.sqrt(head_size)
    flat_ids = jnp.arange(batch_rows * table_width, dtype=jnp.int32)
    inverse = jnp.zeros_like(flat_ids).at[block_table.reshape(-1)].set(flat_ids)
    owner_ids = inverse.reshape(sources, pool_slots)
    owner_rows = owner_ids // table_width
    owner_cols = owner_ids % table_width
    destination = owner_cols // share_blocks * group_count + owner_rows // per_group
    slot_order = jnp.argsort(destination, axis=1, stable=True)
    source_index = seq_index * group_count + group_index
    local_order = lax.dynamic_index_in_dim(slot_order, source_index, 0, keepdims=False)
    outgoing_blocks = jnp.take(cache_pool, local_order, axis=0)
    outgoing_scales = jnp.take(block_scale, local_order, axis=0)
    sent_here = lax.dynamic_slice_in_dim(slot_order, source_index * capacity, capacity, 1)
    arrived_ids = jnp.take_along_axis(owner_ids, sent_here, axis=1).reshape(-1)
    arrived_rows = arrived_ids // table_width - group_index * per_group
    arrived_cols = arrived_ids % table_width - seq_index * share_blocks
    placement = jnp.argsort(arrived_rows * share_blocks + arrived_cols)
    arrived_blocks, arrived_scales = (
        lax.all_to_all(outgoing_blocks, ("seq", "grp"), split_axis=0, concat_axis=0, tiled=True),
        lax.all_to_all(outgoing_scales, ("seq", "grp"), split_axis=0, concat_axis=0, tiled=True),
    )
    decode_cache = jnp.take(arrived_blocks, placement, axis=0).reshape(
        (per_group, share_blocks) + arrived_blocks.shape[1:]
    )
    decode_scale = jnp.take(arrived_scales, placement, axis=0).reshape(
        (per_group, share_blocks) + arrived_scales.shape[1:]
    )
    own_lengths = lax.dynamic_slice_in_dim(lengths, group_index * per_group, per_group)
    block_queries = jnp.broadcast_to(
        queries.reshape(per_group, 1, key_heads, groups, head_size),
        (per_group, share_blocks, key_heads, groups, head_size),
    )
    block_queries = block_queries.reshape(pool_slots, key_heads, groups, head_size)
    block_starts = (
        seq_index * share_blocks + jnp.arange(share_blocks, dtype=jnp.int32)
    ) * block_size
    positions = block_starts[None, :, None] + jnp.arange(block_size, dtype=jnp.int32)[None, None, :]
    live_mask = (positions < own_lengths[:, None, None]).reshape(pool_slots, block_size)
    flat_cache = decode_cache.reshape((pool_slots,) + decode_cache.shape[2:])
    flat_scale = decode_scale.reshape((pool_slots,) + decode_scale.shape[2:]).astype(jnp.float32)
    scores = block_scores(
        block_queries, flat_cache[:, :, 0], flat_scale[:, :, 0], live_mask, root_scale
    )
    request_peak = jnp.max(
        scores.reshape(per_group, share_blocks, key_heads, groups, block_size), axis=(1, 4)
    )
    peak_rows = jnp.broadcast_to(
        request_peak[:, None], (per_group, share_blocks, key_heads, groups)
    )
    peak_rows = peak_rows.reshape(pool_slots, key_heads, groups)
    weight_sum, partial_sum = block_terms(
        scores, peak_rows, live_mask, flat_cache[:, :, 1], flat_scale[:, :, 1]
    )
    request_sum = jnp.sum(weight_sum.reshape(per_group, share_blocks, key_heads, groups), axis=1)
    request_accum = jnp.sum(
        partial_sum.reshape(per_group, share_blocks, key_heads, groups, head_size), axis=1
    )
    peak_all, sum_all, accum_all = joined_all(
        (request_peak, request_sum, request_accum), "seq", combine
    )
    attended = (
        (accum_all / sum_all[..., None])
        .astype(jnp.bfloat16)
        .reshape(per_group, heads_here * head_size)
    )
    partial_out = jnp.dot(
        gather_directly(attended, "grp", 0), output_weight, preferred_element_type=jnp.float32
    )
    summed = sum_at_owner(partial_out, "tp", 0)
    return (summed.astype(jnp.bfloat16), decode_cache, decode_scale)


def solution(mesh):
    placed = (
        P("grp", "tp", None),
        P(("seq", "grp"), "tp", None, None, None),
        P(("seq", "grp"), "tp", None),
        P(),
        P(),
        P("tp", ("seq", "grp")),
    )
    return jax.shard_map(
        per_device,
        mesh=mesh,
        in_specs=placed,
        out_specs=(
            P("tp", ("seq", "grp")),
            P("grp", "seq", "tp", None, None, None),
            P("grp", "seq", "tp", None),
        ),
        check_vma=False,
    )
```

profile of v0, /device:TPU:1, one launch (start us, length us, event | category | flops | bytes accessed | tf_op | source)
XLA Modules:
  0.0 140.6 jit_solution(6368246929354777386)
XLA Ops:
  0.7 0.8 compare_select_fusion
  1.4 8.0 %scatter_custom_fusion = s32[2048]{0:T(1024)S(1)} fusion(s32[2048]{0:T(1024)S(1)} %bitcast.102, s32[2048]{0:T(1024)S(1)} %iota.29, s32[]{:T(128)} %constant.120.clone.1), kind=kCustom, calls=%fused_computation.69 | custom fusion | bytes 8196 | tf_op jit(solution)/shard_map/scatter | solution.py:120
  9.7 1.0 sort.34
  10.7 0.2 dynamic-slice_reduce_fusion
  10.9 0.8 copy.97
  11.9 0.8 gather_fusion
  13.0 0.1 select_n.111
  13.1 0.6 gather_fusion.3
  13.9 0.7 copy.99
  14.6 8.6 %all-to-all-start.1 = ((bf16[64,1,2]{2,1,0:T(2,128)(2,1)}), bf16[64,1,2]{2,1,0:T(2,128)(2,1)S(1)}, u32[]{:S(2)}, u32[]{:S(2)}) async-start(bf16[64,1,2]{2,1,0:T(2,128)(2,1)} %copy.99), calls=%async_computation.1 | async-start | bytes 65536 | tf_op jit(solution)/shard_map/all_to_all | solution.py:137
  23.2 5.3 %gather_fusion.1 = bf16[64,2,128,128]{3,2,1,0:T(8,128)(2,1)} fusion(bf16[64,2,128,128]{3,2,1,0:T(8,128)(2,1)} %bitcast.96, s32[1024]{0:T(1024)S(1)} %pad_clamp_fusion.1), kind=kCustom, calls=%fused_computation.clone | custom fusion | bytes 8388864 | tf_op jit(solution)/shard_map/jit(_take)/gather | solution.py:128
  28.5 4.6 %bitcast_select_fusion.1 = bf16[64,1,2,128,128]{4,3,2,1,0:T(8,128)(2,1)} fusion(bf16[64,2,128,128]{3,2,1,0:T(8,128)(2,1)} %gather_fusion.1, pred[64]{0:T(512)(128)(4,1)S(1)} %compare_and_fusion.1), kind=kLoop, calls=%fused_computation.7 | loop fusion | flops 2097152 | bytes 8388672 | tf_op jit(solution)/shard_map/jit(_take)/select_n | solution.py:128
  33.1 7.6 %all-to-all-start = ((bf16[64,1,2,128,128]{4,3,2,1,0:T(8,128)(2,1)}), bf16[64,1,2,128,128]{4,3,2,1,0:T(8,128)(2,1)}, u32[]{:S(2)}, u32[]{:S(2)}) async-start(bf16[64,1,2,128,128]{4,3,2,1,0:T(8,128)(2,1)} %bitcast_select_fusion.1), calls=%async_computation | async-start | bytes 8388608 | tf_op jit(solution)/shard_map/all_to_all | solution.py:136
  41.0 2.0 %sort.35 = (s32[64]{0:T(128)}, s32[64]{0:T(128)S(1)}) sort(s32[64]{0:T(128)S(1)} %get-tuple-element.46, s32[64]{0:T(128)S(1)} %iota.31), dimensions={0}, to_apply=%region_2.4 | sort | flops 384 | bytes 1024 | tf_op jit(solution)/shard_map/jit(argsort)/sort | solution.py:134
  43.3 0.1 copy.101
  43.4 0.6 gather_fusion.4
  44.1 47.2 %all-to-all-done = bf16[64,1,2,128,128]{4,3,2,1,0:T(8,128)(2,1)} async-done(((bf16[64,1,2,128,128]{4,3,2,1,0:T(8,128)(2,1)}), bf16[64,1,2,128,128]{4,3,2,1,0:T(8,128)(2,1)}, u32[]{:S(2)}, u32[]{:S(2)}) %all-to-all-start) | async-done | bytes 4194336 | tf_op jit(solution)/shard_map/all_to_all | solution.py:136
  91.4 5.3 %gather_fusion.2 = bf16[64,2,128,128]{3,2,1,0:T(8,128)(2,1)} fusion(bf16[64,2,128,128]{3,2,1,0:T(8,128)(2,1)} %bitcast.6, s32[1024]{0:T(1024)S(1)} %pad_clamp_fusion), kind=kCustom, calls=%fused_computation.2.clone | custom fusion | bytes 8388864 | tf_op jit(solution)/shard_map/jit(_take)/gather | solution.py:139
  96.7 2.6 %bitcast_select_fusion = bf16[64,1,2,128,128]{4,3,0,2,1:T(8,128)(2,1)S(1)} fusion(bf16[64,2,128,128]{3,2,1,0:T(8,128)(2,1)} %gather_fusion.2, pred[64]{0:T(512)(128)(4,1)S(1)} %compare_and_fusion), kind=kLoop, calls=%fused_computation.6 | loop fusion | flops 2097152 | bytes 8388672 | tf_op jit(solution)/shard_map/jit(_take)/select_n | solution.py:139
  99.4 1.9 %copy-done.1 = bf16[64,1,2,128,128]{4,3,0,2,1:T(8,128)(2,1)} copy-done((bf16[64,1,2,128,128]{4,3,0,2,1:T(8,128)(2,1)}, bf16[64,1,2,128,128]{4,3,0,2,1:T(8,128)(2,1)S(1)}, u32[]{:S(2)}) %copy-start.1) | copy-done | bytes 4194328
  101.2 1.3 fusion.40
  102.6 0.2 fusion.8
  103.0 2.3 %bitcast_reduce_fusion = f32[2,8,128]{2,1,0:T(8,128)S(1)} fusion(bf16[64,1,2,128,128]{4,3,0,2,1:T(8,128)(2,1)} %copy-done.1, f32[64,8,128]{2,1,0:T(8,128)S(1)} %get-tuple-element.44, f32[64]{0:T(128)S(1)} %get-tuple-element.41, f32[64,8]{1,0:T(8,128)S(1)} %bitcast.99, pred[64,128]{1,0:T(8,128)(4,1)S(1)} %broadcast_compare_fusion), kind=kOutput, calls=%fused_computation.18 | convolution fusion | flops 17102848 | bytes 2377984 | tf_op jit(solution)/shard_map/nkgt,nktd->nkgd/dot_general | solution.py:83
  105.3 8.2 %all_to_all.25 = f32[4,18,128]{2,1,0:T(8,128)S(1)} all-to-all(f32[4,18,128]{2,1,0:T(8,128)S(1)} %broadcast_in_dim.85), channel_id=1, replica_groups=mesh['seq'=4,'tp'=8,'grp'=8] {'seq'}, dimensions={0} | all-to-all | bytes 73728 | tf_op jit(solution)/shard_map/all_to_all | solution.py:13
  114.0 10.4 %all_to_all.26 = bf16[8,2,1024]{2,1,0:T(2,128)(2,1)S(1)} all-to-all(bf16[8,2,1024]{2,1,0:T(2,128)(2,1)S(1)} %broadcast_in_dim.86), channel_id=1, replica_groups=mesh['seq'=4,'tp'=8,'grp'=8] {'grp'}, dimensions={0} | all-to-all | bytes 65536 | tf_op jit(solution)/shard_map/all_to_all | solution.py:13
  124.4 0.2 fusion.6
  124.6 0.6 copy.108
  125.2 8.2 %all-to-all-start.4 = ((f32[8,2,256]{2,1,0:T(2,128)}), f32[8,2,256]{2,1,0:T(2,128)S(1)}, u32[]{:S(2)}, u32[]{:S(2)}) async-start(f32[8,2,256]{2,1,0:T(2,128)} %copy.108), calls=%async_computation.4 | async-start | bytes 32768 | tf_op jit(solution)/shard_map/all_to_all | solution.py:67
  133.4 0.6 copy.110
  134.0 4.8 %copy.109 = bf16[2,32,1,2,128,128]{5,4,3,2,1,0:T(8,128)(2,1)} copy(bf16[2,32,1,2,128,128]{5,4,1,0,3,2:T(8,128)(2,1)} %bitcast.95) | data formatting | bytes 8388608
  138.8 1.2 all-to-all-done.4
  140.0 0.6 reduce_sum.39
  (62 shorter events, 2.3 us)
Async XLA Ops:
  0.6 123.8 %copy-start = (bf16[1024,256]{1,0:T(8,128)(2,1)S(1)}, bf16[1024,256]{1,0:T(8,128)(2,1)}, u32[]{:S(2)}) copy-start(bf16[1024,256]{1,0:T(8,128)(2,1)} %param.15) | copy-start | bytes 1572868
  14.6 18.5 %all-to-all-start.1 = ((bf16[64,1,2]{2,1,0:T(2,128)(2,1)}), bf16[64,1,2]{2,1,0:T(2,128)(2,1)S(1)}, u32[]{:S(2)}, u32[]{:S(2)}) async-start(bf16[64,1,2]{2,1,0:T(2,128)(2,1)} %copy.99), calls=%async_computation.1 | async-start | bytes 65536 | tf_op jit(solution)/shard_map/all_to_all | solution.py:137
  33.1 7.6 %copy-start.3 = (s32[16]{0:T(128)S(1)}, s32[16]{0:T(128)}, u32[]{:S(2)}) copy-start(s32[16]{0:T(128)} %param.14) | copy-start | bytes 196
  33.1 58.3 %all-to-all-start = ((bf16[64,1,2,128,128]{4,3,2,1,0:T(8,128)(2,1)}), bf16[64,1,2,128,128]{4,3,2,1,0:T(8,128)(2,1)}, u32[]{:S(2)}, u32[]{:S(2)}) async-start(bf16[64,1,2,128,128]{4,3,2,1,0:T(8,128)(2,1)} %bitcast_select_fusion.1), calls=%async_computation | async-start | bytes 8388608 | tf_op jit(solution)/shard_map/all_to_all | solution.py:136
  96.7 2.7 %copy-start.2 = (bf16[2,8,128]{2,1,0:T(8,128)(2,1)S(1)}, bf16[2,8,128]{2,1,0:T(8,128)(2,1)}, u32[]{:S(2)}) copy-start(bf16[2,8,128]{2,1,0:T(8,128)(2,1)} %param.10) | copy-start | bytes 12292
  99.3 1.9 %copy-start.1 = (bf16[64,1,2,128,128]{4,3,0,2,1:T(8,128)(2,1)}, bf16[64,1,2,128,128]{4,3,0,2,1:T(8,128)(2,1)S(1)}, u32[]{:S(2)}) copy-start(bf16[64,1,2,128,128]{4,3,0,2,1:T(8,128)(2,1)S(1)} %bitcast_select_fusion) | copy-start | bytes 12582916
  125.2 14.8 %all-to-all-start.4 = ((f32[8,2,256]{2,1,0:T(2,128)}), f32[8,2,256]{2,1,0:T(2,128)S(1)}, u32[]{:S(2)}, u32[]{:S(2)}) async-start(f32[8,2,256]{2,1,0:T(2,128)} %copy.108), calls=%async_computation.4 | async-start | bytes 32768 | tf_op jit(solution)/shard_map/all_to_all | solution.py:67
where the time goes:
time: 141 us
  waiting for transfers between devices  48.4 us (34%)
  local copies, waits for them, and re-layouts  32.1 us (23%)
  starting transfers between devices  24.3 us (17%)
  blocking collectives  18.6 us (13%)
  other arithmetic  12.5 us (9%)
  matrix products  3.74 us (3%)
    all_to_all x1, waiting for transfers between devices, per_device(): lax.all_to_all(outgoing_blocks, ('seq', 'grp'), split_axis=0, concat_axis...  47.2 us
    all_to_all x2, blocking collectives, sent_to_all(): lax.all_to_all(jnp.broadcast_to(array[None], (length, *array.shape)), axi...  18.6 us
    all_to_all x1, starting transfers between devices, per_device(): lax.all_to_all(outgoing_scales, ('seq', 'grp'), split_axis=0, concat_axis...  8.58 us
    all_to_all x1, starting transfers between devices, sum_at_owner(): lax.all_to_all(pieces, axis, split_axis=0, concat_axis=0, tiled=True)  8.19 us
    scatter x1, local copies, waits for them, and re-layouts, per_device(): inverse = jnp.zeros_like(flat_ids).at[block_table.reshape(-1)].set(flat_ids)  8.05 us
    all_to_all x1, starting transfers between devices, per_device(): lax.all_to_all(outgoing_blocks, ('seq', 'grp'), split_axis=0, concat_axis...  7.57 us
    unnamed x11, local copies, waits for them, and re-layouts  7.33 us
    gather x1, local copies, waits for them, and re-layouts, per_device(): outgoing_blocks = jnp.take(cache_pool, local_order, axis=0)  5.29 us
  transfers between devices with their start and end apart: 3, of which 2 were waited for; matrix products, arithmetic and copies ran while one was open for 13% of the time, Pallas kernels for 0%

commit v1 on v0

--- a/solution.py
+++ b/solution.py
@@ -1,11 +1,17 @@
+import functools
 import math
 
 import jax
 import jax.numpy as jnp
 from jax import lax
+from jax.experimental import pallas as pl
+from jax.experimental.pallas import tpu as pltpu
 from jax.sharding import PartitionSpec as P
 
 absent_score = -1e30
+both_axes = ("seq", "grp")
+far = 1 << 20
+scale_rows = 8
 
 
 def sent_to_all(array, axis):
@@ -99,6 +105,104 @@
     )
 
 
+def outgoing_codes(block_table, source, slots, groups, ranges):
+    rows, width = block_table.shape
+    per_group, span = rows // groups, width // ranges
+    table = block_table.reshape(groups, per_group, width)
+    column = lax.broadcasted_iota(jnp.int32, table.shape, 2)
+    row = lax.broadcasted_iota(jnp.int32, table.shape, 1)
+    code = (row * span + column % span) * slots + table % slots
+    mine = (table // slots == source)[:, :, None, :] & (
+        (column // span)[:, :, None, :] == jnp.arange(ranges, dtype=jnp.int32)[None, None, :, None]
+    )
+    code = jnp.broadcast_to(code[:, :, None, :], mine.shape)
+    return (
+        jnp.min(jnp.where(mine, code, far), axis=(1, 3)),
+        jnp.max(jnp.where(mine, code, -1), axis=(1, 3)),
+    )
+
+
+def arrival_places(block_table, seq_index, group_index, slots, groups, ranges):
+    rows, width = block_table.shape
+    per_group, span = rows // groups, width // ranges
+    own = lax.dynamic_slice(
+        block_table, (group_index * per_group, seq_index * span), (per_group, span)
+    )
+    source = (own // slots)[None]
+    place = lax.broadcasted_iota(jnp.int32, (1, per_group, span), 1) * span
+    place = place + lax.broadcasted_iota(jnp.int32, (1, per_group, span), 2)
+    here = source == jnp.arange(groups * ranges, dtype=jnp.int32)[:, None, None]
+    return (
+        jnp.min(jnp.where(here, place, far), axis=(1, 2)),
+        jnp.max(jnp.where(here, place, -1), axis=(1, 2)),
+    )
+
+
+def gather_kernel(groups, ranges, slots, first, second, scales, pool, out, held, in_sem, out_sem):
+    rows = pool.shape[1]
+    copies = []
+    for s in range(ranges):
+        for g in range(groups):
+            d = s * groups + g
+            for k, codes in enumerate((first, second)):
+                slot = lax.rem(codes[g, s], slots)
+                copy = pltpu.make_async_copy(
+                    pool.at[slot], held.at[d, pl.ds(k * rows, rows)], in_sem.at[2 * d + k]
+                )
+                copy.start()
+                copies.append(copy)
+    row = lax.broadcasted_iota(jnp.int32, (scale_rows, 128), 0)
+    lane = lax.broadcasted_iota(jnp.int32, (scale_rows, 128), 1)
+    for s in range(ranges):
+        for g in range(groups):
+            d = s * groups + g
+            one, two = (lax.rem(codes[g, s], slots) for codes in (first, second))
+            keys = jnp.where(row == 0, scales[2 * one], scales[2 * two])
+            values = jnp.where(row == 0, scales[2 * one + 1], scales[2 * two + 1])
+            held[d, pl.ds(2 * rows, scale_rows)] = jnp.where(lane == 0, keys, values).astype(
+                held.dtype
+            )
+    sent = []
+    for d in range(groups * ranges):
+        for k in range(2):
+            copies[2 * d + k].wait()
+        copy = pltpu.make_async_copy(held.at[d], out.at[d], out_sem.at[d])
+        copy.start()
+        sent.append(copy)
+    for copy in sent:
+        copy.wait()
+
+
+def place_kernel(first, second, arrived, cache, scale, held, in_sem, out_sem):
+    sources = arrived.shape[0]
+    rows = cache.shape[1]
+    copies = []
+    for d in range(sources):
+        copy = pltpu.make_async_copy(arrived.at[d], held.at[d], in_sem.at[d])
+        copy.start()
+        copies.append(copy)
+    sent = []
+    for d in range(sources):
+        copies[d].wait()
+        for k, places in enumerate((first, second)):
+            copy = pltpu.make_async_copy(
+                held.at[d, pl.ds(k * rows, rows)], cache.at[places[d]], out_sem.at[2 * d + k]
+            )
+            copy.start()
+            sent.append(copy)
+        tile = held[d, pl.ds(2 * rows, scale_rows)].astype(jnp.float32)
+        for k, places in enumerate((first, second)):
+            scale[pl.ds(places[d], 1), :] = tile[k : k + 1]
+    for copy in sent:
+        copy.wait()
+
+
+smem = pl.BlockSpec(memory_space=pltpu.SMEM)
+vmem = pl.BlockSpec(memory_space=pltpu.VMEM)
+anywhere = pl.BlockSpec(memory_space=pl.ANY)
+small_grant = 16 * 1024 * 1024
+
+
 def per_device(queries, cache_pool, block_scale, block_table, lengths, output_weight):
     seq_count = lax.axis_size("seq")
     group_count = lax.axis_size("grp")
@@ -112,35 +216,54 @@
     batch_rows, table_width = block_table.shape
     per_group = batch_rows // group_count
     share_blocks = table_width // seq_count
-    capacity = pool_slots // sources
     heads_here = queries.shape[1]
     groups = heads_here // key_heads
     root_scale = 1.0 / math.sqrt(head_size)
-    flat_ids = jnp.arange(batch_rows * table_width, dtype=jnp.int32)
-    inverse = jnp.zeros_like(flat_ids).at[block_table.reshape(-1)].set(flat_ids)
-    owner_ids = inverse.reshape(sources, pool_slots)
-    owner_rows = owner_ids // table_width
-    owner_cols = owner_ids % table_width
-    destination = owner_cols // share_blocks * group_count + owner_rows // per_group
-    slot_order = jnp.argsort(destination, axis=1, stable=True)
+    rows = 2 * block_size
     source_index = seq_index * group_count + group_index
-    local_order = lax.dynamic_index_in_dim(slot_order, source_index, 0, keepdims=False)
-    outgoing_blocks = jnp.take(cache_pool, local_order, axis=0)
-    outgoing_scales = jnp.take(block_scale, local_order, axis=0)
-    sent_here = lax.dynamic_slice_in_dim(slot_order, source_index * capacity, capacity, 1)
-    arrived_ids = jnp.take_along_axis(owner_ids, sent_here, axis=1).reshape(-1)
-    arrived_rows = arrived_ids // table_width - group_index * per_group
-    arrived_cols = arrived_ids % table_width - seq_index * share_blocks
-    placement = jnp.argsort(arrived_rows * share_blocks + arrived_cols)
-    arrived_blocks, arrived_scales = (
-        lax.all_to_all(outgoing_blocks, ("seq", "grp"), split_axis=0, concat_axis=0, tiled=True),
-        lax.all_to_all(outgoing_scales, ("seq", "grp"), split_axis=0, concat_axis=0, tiled=True),
-    )
-    decode_cache = jnp.take(arrived_blocks, placement, axis=0).reshape(
-        (per_group, share_blocks) + arrived_blocks.shape[1:]
-    )
-    decode_scale = jnp.take(arrived_scales, placement, axis=0).reshape(
-        (per_group, share_blocks) + arrived_scales.shape[1:]
+    first, second = outgoing_codes(block_table, source_index, pool_slots, group_count, seq_count)
+    tall = 2 * rows + scale_rows
+    outgoing = pl.pallas_call(
+        functools.partial(gather_kernel, group_count, seq_count, pool_slots),
+        out_shape=jax.ShapeDtypeStruct((sources, tall, head_size), cache_pool.dtype),
+        in_specs=[smem, smem, smem, anywhere],
+        out_specs=anywhere,
+        scratch_shapes=[
+            pltpu.VMEM((sources, tall, head_size), cache_pool.dtype),
+            pltpu.SemaphoreType.DMA((2 * sources,)),
+            pltpu.SemaphoreType.DMA((sources,)),
+        ],
+        compiler_params=pltpu.CompilerParams(vmem_limit_bytes=small_grant),
+    )(
+        first,
+        second,
+        block_scale.astype(jnp.float32).reshape(-1),
+        cache_pool.reshape(pool_slots, rows, head_size),
+    )
+    arrived = lax.all_to_all(outgoing, both_axes, split_axis=0, concat_axis=0, tiled=True)
+    first_place, second_place = arrival_places(
+        block_table, seq_index, group_index, pool_slots, group_count, seq_count
+    )
+    placed, scale_lines = pl.pallas_call(
+        place_kernel,
+        out_shape=(
+            jax.ShapeDtypeStruct((pool_slots, rows, head_size), cache_pool.dtype),
+            jax.ShapeDtypeStruct((pool_slots, 128), jnp.float32),
+        ),
+        in_specs=[smem, smem, anywhere],
+        out_specs=(anywhere, vmem),
+        scratch_shapes=[
+            pltpu.VMEM((sources, tall, head_size), cache_pool.dtype),
+            pltpu.SemaphoreType.DMA((sources,)),
+            pltpu.SemaphoreType.DMA((2 * sources,)),
+        ],
+        compiler_params=pltpu.CompilerParams(vmem_limit_bytes=small_grant),
+    )(first_place, second_place, arrived)
+    decode_cache = placed.reshape(
+        per_group, share_blocks, key_heads, 2, block_size, head_size
+    )
+    decode_scale = (
+        scale_lines[:, :2].astype(block_scale.dtype).reshape(per_group, share_blocks, key_heads, 2)
     )
     own_lengths = lax.dynamic_slice_in_dim(lengths, group_index * per_group, per_group)
     block_queries = jnp.broadcast_to(
@@ -154,7 +277,7 @@
     positions = block_starts[None, :, None] + jnp.arange(block_size, dtype=jnp.int32)[None, None, :]
     live_mask = (positions < own_lengths[:, None, None]).reshape(pool_slots, block_size)
     flat_cache = decode_cache.reshape((pool_slots,) + decode_cache.shape[2:])
-    flat_scale = decode_scale.reshape((pool_slots,) + decode_scale.shape[2:]).astype(jnp.float32)
+    flat_scale = scale_lines[:, :2].reshape(pool_slots, key_heads, 2)
     scores = block_scores(
         block_queries, flat_cache[:, :, 0], flat_scale[:, :, 0], live_mask, root_scale
     )

time: 141 us -> 128 us (0.908)
  local copies, waits for them, and re-layouts: 32.1 us -> 7.31 us
  Pallas kernels: 0 us -> 18.5 us
  other arithmetic: 12.5 us -> 3.92 us
  waiting for transfers between devices: 48.4 us -> 56 us
  starting transfers between devices: 24.3 us -> 16.9 us
  matrix products: 3.74 us -> 5.37 us
    pallas_call x0 -> x2, Pallas kernels: none -> 18.5 us  [the longest x1 13 us: per_device(): pl.pallas_call(functools.partial(gather_kernel, group_count, seq_count, p...]
    gather x11 -> x0, local copies, waits for them, and re-layouts: 13.2 us -> none  [the longest x1 5.29 us: per_device(): outgoing_blocks = jnp.take(cache_pool, local_order, axis=0)]
    scatter x1 -> x0, local copies, waits for them, and re-layouts: 8.05 us -> none  [per_device(): inverse = jnp.zeros_like(flat_ids).at[block_table.reshape(-1)].set(flat_ids)]
    all_to_all x2 -> x1, starting transfers between devices: 16.1 us -> 8.76 us  [per_device(): lax.all_to_all(outgoing, both_axes, split_axis=0, concat_axis=0, tiled=True)]
    select_n x7 -> x2, other arithmetic: 8.08 us -> 0.78 us  [the longest x1 0.77 us: arrival_places(): source = (own // slots)[None]]
    all_to_all x1, waiting for transfers between devices: 1.18 us -> 5.96 us  [sum_at_owner(): lax.all_to_all(pieces, axis, split_axis=0, concat_axis=0, tiled=True)]
    sort x2 -> x0, other arithmetic: 3.06 us -> none  [the longest x1 2.04 us: per_device(): placement = jnp.argsort(arrived_rows * share_blocks + arrived_cols)]
    all_to_all x2 -> x1, waiting for transfers between devices: 47.2 us -> 50 us  [per_device(): lax.all_to_all(outgoing, both_axes, split_axis=0, concat_axis=0, tiled=True)]
  transfers between devices with their start and end apart: 3 -> 2, of which waited for: 2 -> 2; matrix products, arithmetic and copies ran while one was open for 13% -> 2% of each run, Pallas kernels for 0% -> 0%
where the time goes in v1:
time: 128 us
  waiting for transfers between devices  56 us (44%)
  blocking collectives  18.6 us (15%)
  Pallas kernels  18.5 us (14%)
  starting transfers between devices  16.9 us (13%)
  local copies, waits for them, and re-layouts  7.31 us (6%)
  matrix products  5.37 us (4%)
  other arithmetic  3.92 us (3%)
    all_to_all x1, waiting for transfers between devices, per_device(): lax.all_to_all(outgoing, both_axes, split_axis=0, concat_axis=0, tiled=True)  50 us
    all_to_all x2, blocking collectives, sent_to_all(): lax.all_to_all(jnp.broadcast_to(array[None], (length, *array.shape)), axi...  18.6 us
    pallas_call x1, Pallas kernels, per_device(): pl.pallas_call(functools.partial(gather_kernel, group_count, seq_count, p...  13 us
    all_to_all x1, starting transfers between devices, per_device(): lax.all_to_all(outgoing, both_axes, split_axis=0, concat_axis=0, tiled=True)  8.76 us
    all_to_all x1, starting transfers between devices, sum_at_owner(): lax.all_to_all(pieces, axis, split_axis=0, concat_axis=0, tiled=True)  8.19 us
    all_to_all x1, waiting for transfers between devices, sum_at_owner(): lax.all_to_all(pieces, axis, split_axis=0, concat_axis=0, tiled=True)  5.96 us
    pallas_call x1, Pallas kernels, per_device(): pl.pallas_call(place_kernel, out_shape=(jax.ShapeDtypeStruct((pool_slots,...  5.44 us
    unnamed x12, local copies, waits for them, and re-layouts  4.93 us
  transfers between devices with their start and end apart: 2, of which 2 were waited for; matrix products, arithmetic and copies ran while one was open for 2% of the time, Pallas kernels for 0%

profile of v1, /device:TPU:1, one launch (start us, length us, event | category | flops | bytes accessed | tf_op | source)
XLA Modules:
  0.0 127.5 jit_solution(16724772180548416585)
XLA Ops:
  0.7 0.8 fusion.15
  1.5 0.8 fusion.16
  2.3 0.2 select_reduce_fusion
  2.5 0.1 copy.101.first
  2.6 0.1 copy.102.second
  2.6 0.8 copy.100
  3.4 0.1 reshape.287.scales
  3.5 2.2 %copy-done.2 = bf16[64,1,2,128,128]{4,3,2,1,0:T(8,128)(2,1)S(1)} copy-done((bf16[64,1,2,128,128]{4,3,2,1,0:T(8,128)(2,1)S(1)}, bf16[64,1,2,128,128]{4,3,2,1,0:T(8,128)(2,1)}, u32[]{:S(2)}) %copy-start.2) | copy-done | bytes 4194328
  5.7 13.0 %shard_map.85 = bf16[32,520,128]{2,1,0:T(8,128)(2,1)S(1)} custom-call(s32[8,4]{1,0:T(8,128)S(1)} %copy.101.first, s32[8,4]{1,0:T(8,128)S(1)} %copy.102.second, f32[128]{0:T(128)S(1)} %reshape.287.scales, bf16[64,256,128]{2,1,0:T(8,128)(2,1)S(1)} %bitcast.88), custom_call_target="tpu_custom_call" | custom-call | tf_op jit(solution)/shard_map/pallas_call | solution.py:226
  18.8 2.0 %copy-done.1 = bf16[32,520,128]{2,1,0:T(8,128)(2,1)} copy-done((bf16[32,520,128]{2,1,0:T(8,128)(2,1)}, bf16[32,520,128]{2,1,0:T(8,128)(2,1)S(1)}, u32[]{:S(2)}) %copy-start.1) | copy-done | bytes 4259864
  20.8 8.8 %all-to-all-start = ((bf16[32,520,128]{2,1,0:T(8,128)(2,1)}), bf16[32,520,128]{2,1,0:T(8,128)(2,1)}, u32[]{:S(2)}, u32[]{:S(2)}) async-start(bf16[32,520,128]{2,1,0:T(8,128)(2,1)} %copy-done.1), calls=%async_computation | async-start | bytes 8519680 | tf_op jit(solution)/shard_map/all_to_all | solution.py:243
  29.6 0.1 dynamic_slice.6
  29.7 0.1 lt.45
  30.0 0.8 and_select_fusion
  30.8 0.1 select_reduce_fusion.2
  30.9 50.0 %all-to-all-done.arrived = bf16[32,520,128]{2,1,0:T(8,128)(2,1)} async-done(((bf16[32,520,128]{2,1,0:T(8,128)(2,1)}), bf16[32,520,128]{2,1,0:T(8,128)(2,1)}, u32[]{:S(2)}, u32[]{:S(2)}) %all-to-all-start) | async-done | bytes 4259872 | tf_op jit(solution)/shard_map/all_to_all | solution.py:243
  80.9 5.4 %shard_map.86 = (bf16[64,256,128]{2,1,0:T(8,128)(2,1)}, f32[64,128]{1,0:T(8,128)S(1)}) custom-call(s32[32]{0:T(128)S(1)} %get-tuple-element.34.first, s32[32]{0:T(128)S(1)} %get-tuple-element.33.second, bf16[32,520,128]{2,1,0:T(8,128)(2,1)} %all-to-all-done.arrived), custom_call_target="tpu_custom_call" | custom-call | tf_op jit(solution)/shard_map/pallas_call | solution.py:247
  86.5 2.9 %fusion.32 = (f32[64,8]{1,0:T(8,128)S(1)}, f32[64,8,128]{2,1,0:T(8,128)S(1)}) fusion(f32[64]{0:T(128)S(1)} %get-tuple-element.45, bf16[64,8,128]{2,1,0:T(8,128)(2,1)S(1)} %bitcast.90, bf16[64,1,2,128,128]{4,3,2,0,1:T(8,128)(2,1)} %bitcast.100, pred[64,128]{1,0:T(8,128)(4,1)S(1)} %broadcast_compare_fusion), kind=kOutput, calls=%fused_computation.89 | convolution fusion | flops 17038848 | bytes 2500864 | tf_op jit(solution)/shard_map/nkgd,nktd->nkgt/dot_general | solution.py:78
  89.4 0.1 reshape.275
  89.5 0.2 fusion.8
  89.7 2.3 %bitcast_reduce_fusion = f32[2,8,128]{2,1,0:T(8,128)S(1)} fusion(bf16[64,1,2,128,128]{4,3,2,0,1:T(8,128)(2,1)} %bitcast.101, f32[64,8,128]{2,1,0:T(8,128)S(1)} %get-tuple-element.47, f32[64]{0:T(128)S(1)} %get-tuple-element.44, f32[64,8]{1,0:T(8,128)S(1)} %bitcast.92, pred[64,128]{1,0:T(8,128)(4,1)S(1)} %broadcast_compare_fusion), kind=kOutput, calls=%fused_computation.10 | convolution fusion | flops 17102848 | bytes 2377984 | tf_op jit(solution)/shard_map/nkgt,nktd->nkgd/dot_general | solution.py:89
  92.0 0.1 reshape.278
  92.2 8.2 %all_to_all.20 = f32[4,18,128]{2,1,0:T(8,128)S(1)} all-to-all(f32[4,18,128]{2,1,0:T(8,128)S(1)} %broadcast_in_dim.105), channel_id=1, replica_groups=mesh['seq'=4,'tp'=8,'grp'=8] {'seq'}, dimensions={0} | all-to-all | bytes 73728 | tf_op jit(solution)/shard_map/all_to_all | solution.py:19
  100.4 0.1 reshape.281
  100.5 0.1 reshape.283
  100.9 10.5 %all_to_all.21 = bf16[8,2,1024]{2,1,0:T(2,128)(2,1)S(1)} all-to-all(bf16[8,2,1024]{2,1,0:T(2,128)(2,1)S(1)} %broadcast_in_dim.106), channel_id=1, replica_groups=mesh['seq'=4,'tp'=8,'grp'=8] {'grp'}, dimensions={0} | all-to-all | bytes 65536 | tf_op jit(solution)/shard_map/all_to_all | solution.py:19
  111.3 0.2 fusion.6
  111.5 0.6 copy.111
  112.1 8.2 %all-to-all-start.3 = ((f32[8,2,256]{2,1,0:T(2,128)}), f32[8,2,256]{2,1,0:T(2,128)S(1)}, u32[]{:S(2)}, u32[]{:S(2)}) async-start(f32[8,2,256]{2,1,0:T(2,128)} %copy.111), calls=%async_computation.3 | async-start | bytes 32768 | tf_op jit(solution)/shard_map/all_to_all | solution.py:73
  120.3 0.7 copy.114
  121.0 6.0 %all-to-all-done.3 = f32[8,2,256]{2,1,0:T(2,128)S(1)} async-done(((f32[8,2,256]{2,1,0:T(2,128)}), f32[8,2,256]{2,1,0:T(2,128)S(1)}, u32[]{:S(2)}, u32[]{:S(2)}) %all-to-all-start.3) | async-done | bytes 16416 | tf_op jit(solution)/shard_map/all_to_all | solution.py:73
  126.9 0.6 reduce_sum.39
  (39 shorter events, 0.8 us)
Async XLA Ops:
  0.6 110.7 %copy-start = (bf16[1024,256]{1,0:T(8,128)(2,1)S(1)}, bf16[1024,256]{1,0:T(8,128)(2,1)}, u32[]{:S(2)}) copy-start(bf16[1024,256]{1,0:T(8,128)(2,1)} %param.11) | copy-start | bytes 1572868
  3.5 2.2 %copy-start.2 = (bf16[64,1,2,128,128]{4,3,2,1,0:T(8,128)(2,1)S(1)}, bf16[64,1,2,128,128]{4,3,2,1,0:T(8,128)(2,1)}, u32[]{:S(2)}) copy-start(bf16[64,1,2,128,128]{4,3,2,1,0:T(8,128)(2,1)} %param.7) | copy-start | bytes 12582916
  18.8 2.0 %copy-start.1 = (bf16[32,520,128]{2,1,0:T(8,128)(2,1)}, bf16[32,520,128]{2,1,0:T(8,128)(2,1)S(1)}, u32[]{:S(2)}) copy-start(bf16[32,520,128]{2,1,0:T(8,128)(2,1)S(1)} %shard_map.85) | copy-start | bytes 12779524
  20.8 8.8 %copy-start.4 = (s32[16]{0:T(128)S(1)}, s32[16]{0:T(128)}, u32[]{:S(2)}) copy-start(s32[16]{0:T(128)} %param.10) | copy-start | bytes 196
  20.8 60.1 %all-to-all-start = ((bf16[32,520,128]{2,1,0:T(8,128)(2,1)}), bf16[32,520,128]{2,1,0:T(8,128)(2,1)}, u32[]{:S(2)}, u32[]{:S(2)}) async-start(bf16[32,520,128]{2,1,0:T(8,128)(2,1)} %copy-done.1), calls=%async_computation | async-start | bytes 8519680 | tf_op jit(solution)/shard_map/all_to_all | solution.py:243
  29.6 56.9 %copy-start.3 = (bf16[2,8,128]{2,1,0:T(8,128)(2,1)S(1)}, bf16[2,8,128]{2,1,0:T(8,128)(2,1)}, u32[]{:S(2)}) copy-start(bf16[2,8,128]{2,1,0:T(8,128)(2,1)} %param.6) | copy-start | bytes 12292
  112.1 14.8 %all-to-all-start.3 = ((f32[8,2,256]{2,1,0:T(2,128)}), f32[8,2,256]{2,1,0:T(2,128)S(1)}, u32[]{:S(2)}, u32[]{:S(2)}) async-start(f32[8,2,256]{2,1,0:T(2,128)} %copy.111), calls=%async_computation.3 | async-start | bytes 32768 | tf_op jit(solution)/shard_map/all_to_all | solution.py:73
